TPU v7x, 32 devices: a whole 2x2x4 slice. The times are simulated.
32 devices in a mesh: row: 8 (over z, x), col: 4 (over y, core).
Axes of the slice: x: 2, y: 2, z: 4, core: 2. Of those that a mesh axis runs over, the one named last changes fastest.
Arguments:
- normal_matrix: float32 [4096, 4096], P('row', 'col'), as said below
Outputs:
- factored: float32 [4096, 4096], P('row', 'col')
- log_det: float32 [], replicated
Inputs may be any that keep to these rules, and one draw needn't show every extreme that they name: normal_matrix is symmetric and positive definite.
All inputs are finite; a program needn't handle non-finite values.
Results may differ from a plain program's by a relative error of at most 0.0001.
Values sent between devices are 32-bit elements; how exact they have to be, the bound alone decides.
A program may use at most 64 MiB of HBM per device.

v0:
```python
import functools

import jax
import jax.numpy as jnp
from jax import lax
from jax.experimental import pallas as pl
from jax.experimental.pallas import tpu as pltpu
from jax.sharding import PartitionSpec as P

MESH = pl.DeviceIdType.MESH
NB = 128
CHUNKS = 4
VMEM = pl.BlockSpec(memory_space=pltpu.VMEM)


def dot_nt(a, b):
    return lax.dot_general(
        a, b, (((1,), (1,)), ((), ())), precision=lax.Precision.HIGHEST,
        preferred_element_type=jnp.float32,
    )


def dot_nn(a, b):
    return lax.dot_general(
        a, b, (((1,), (0,)), ((), ())), precision=lax.Precision.HIGHEST,
        preferred_element_type=jnp.float32,
    )


def factor_block(a):
    groups = NB // 8
    lane = lax.broadcasted_iota(jnp.int32, (8, NB), 1)
    sub = lax.broadcasted_iota(jnp.int32, (8, NB), 0)
    left = [a[8 * g : 8 * g + 8, :] for g in range(groups)]
    right = [(lane == sub + 8 * g).astype(jnp.float32) for g in range(groups)]
    upper, inverse, pivots = [], [], []

    def row(x, t):
        return jnp.broadcast_to(x[t : t + 1, :], (8, NB))

    def column(x, t):
        return jnp.broadcast_to(x[:, t : t + 1], (8, NB))

    for p in range(groups):
        first = 8 * p
        v, i = left[p], right[p]
        cols = [column(v, first + t) for t in range(8)]
        mult = {g: [column(left[g], first + t) for t in range(8)] for g in range(p + 1, groups)}
        u_rows, i_rows, d_rows = v, i, cols[0]
        for t in range(8):
            here = sub == t
            pivot = row(cols[t], t)
            if t:
                u_rows = jnp.where(here, v, u_rows)
                i_rows = jnp.where(here, i, i_rows)
            d_rows = jnp.where(here, pivot, d_rows)
            recip = 1.0 / pivot
            factor = jnp.where(here, -recip, cols[t] * recip)
            for u in range(t + 1, 8):
                cols[u] = jnp.where(here, 0.0, cols[u]) - factor * row(cols[u], t)
            v = jnp.where(here, 0.0, v) - factor * row(v, t)
            i = jnp.where(here, 0.0, i) - factor * row(i, t)
        scale = lax.rsqrt(d_rows)
        upper.append(jnp.where(lane >= sub + first, u_rows * scale, 0.0))
        inverse.append(i_rows * scale)
        pivots.append(d_rows)
        v_rows = [row(v, t) for t in range(8)]
        i_rows = [row(i, t) for t in range(8)]
        for g in range(p + 1, groups):
            left_sum = mult[g][0] * v_rows[0]
            right_sum = mult[g][0] * i_rows[0]
            for t in range(1, 8):
                left_sum = left_sum + mult[g][t] * v_rows[t]
                right_sum = right_sum + mult[g][t] * i_rows[t]
            left[g] = left[g] - left_sum
            right[g] = right[g] - right_sum
    return jnp.concatenate(upper, 0), jnp.concatenate(inverse, 0), jnp.concatenate(pivots, 0)


def cholesky_kernel(a_ref, l_ref, w_ref, logdet_ref, work, upper, inverse, pivot):
    size = a_ref.shape[0]
    work[...] = a_ref[...]
    l_ref[...] = jnp.zeros_like(l_ref)
    w_ref[...] = jnp.zeros_like(w_ref)

    @pl.loop(0, size // NB)
    def _(step):
        span = pl.ds(pl.multiple_of(step * NB, NB), NB)
        r, w, d = factor_block(work[span, span])
        upper[...] = r
        inverse[...] = w
        pivot[span, :] = d
        w_ref[span, span] = inverse[...]
        l_ref[span, span] = upper[...].T
        for p in range(size // NB):

            @pl.when(step == p)
            def _():
                at = slice(p * NB, (p + 1) * NB)
                end = (p + 1) * NB
                if p:
                    inner = dot_nn(l_ref[at, : p * NB], w_ref[: p * NB, : p * NB])
                    w_ref[at, : p * NB] = -dot_nn(inverse[...], inner)
                if end < size:
                    panel = dot_nt(work[end:, at], inverse[...])
                    l_ref[end:, at] = panel
                    work[end:, end:] = work[end:, end:] - dot_nt(panel, panel)

    logdet_ref[...] = jnp.sum(jnp.log(pivot[...]), axis=0, keepdims=True)


def cholesky(a):
    size = a.shape[0]
    square = jax.ShapeDtypeStruct((size, size), jnp.float32)
    return pl.pallas_call(
        cholesky_kernel,
        out_shape=(square, square, jax.ShapeDtypeStruct((1, NB), jnp.float32)),
        in_specs=[VMEM],
        out_specs=(VMEM, VMEM, VMEM),
        scratch_shapes=[
            pltpu.VMEM((size, size), jnp.float32),
            pltpu.VMEM((NB, NB), jnp.float32),
            pltpu.VMEM((NB, NB), jnp.float32),
            pltpu.VMEM((size, NB), jnp.float32),
        ],
    )(a)


def update_kernel(mine_ref, own_ref, cols_ref, w_ref, l_ref, out_ref):
    r, c = lax.axis_index("row"), lax.axis_index("col")
    width = own_ref.shape[0]

    @pl.when(r == 0)
    def _():
        out_ref[...] = jnp.zeros_like(out_ref)

        @pl.when(c == 0)
        def _():
            out_ref[:, :width] = l_ref[...]

    @pl.when(r > 0)
    def _():
        panel = dot_nt(own_ref[...], w_ref[...])
        for slot in range(2):
            at = slice(slot * width, (slot + 1) * width)
            other = dot_nt(cols_ref[at, :], w_ref[...])
            out_ref[:, at] = mine_ref[:, at] - dot_nt(panel, other)

        @pl.when(c == 0)
        def _():
            out_ref[:, :width] = panel


def gather_kernel(mine_ref, own_ref, diag_ref, cols_ref, load_sem, own_send, own_recv,
                  diag_send, diag_recv, cols_send, cols_recv, keep_sem):
    rows, columns = lax.axis_size("row"), lax.axis_size("col")
    r, c = lax.axis_index("row"), lax.axis_index("col")
    q, x = r // 2, r % 2
    other = r + 1 - 2 * x
    width = own_ref.shape[0]
    piece = width // CHUNKS
    even = c % 2 == 0

    links = [
        ((r, c - 1), c >= 1), ((r, c + 1), c + 1 < columns),
        ((r, c - 2), c >= 2), ((r, c + 2), c + 2 < columns),
        ((r - 2, c), r >= 2), ((r + 2, c), r + 2 < rows),
        ((other, c), other >= 0),
    ]
    barrier = pltpu.get_barrier_semaphore()
    for device, exists in links:
        @pl.when(exists)
        def _():
            pl.semaphore_signal(barrier, inc=1, device_id=device, device_id_type=MESH)
    peers = sum(jnp.where(exists, 1, 0).astype(jnp.int32) for _, exists in links)
    pl.semaphore_wait(barrier, peers)

    def part(ref, i, base=0):
        return ref.at[pl.ds(base + i * piece, piece), :]

    def send(source, target, send_sem, recv_sem, device):
        return pltpu.make_async_remote_copy(
            src_ref=source, dst_ref=target, send_sem=send_sem, recv_sem=recv_sem,
            device_id=device, device_id_type=MESH,
        )

    def load(i):
        return pltpu.make_async_copy(
            mine_ref.at[pl.ds(i * piece, piece), pl.ds(0, width)], part(own_ref, i), load_sem.at[i]
        )

    base_x = pl.multiple_of(x * width, width)
    base_o = pl.multiple_of((1 - x) * width, width)
    sends = []

    def forward(condition, *args):
        copy = send(*args)
        sends.append((condition, copy))

        @pl.when(condition)
        def _():
            copy.start()

    def own_part(i):
        return send(part(own_ref, i), part(own_ref, i), own_send.at[0, i], own_recv.at[i], (r, c + 1))

    @pl.when(c == 0)
    def _():
        for i in range(CHUNKS):
            load(i).start()

    keeps = []
    for i in range(CHUNKS):
        @pl.when(c == 0)
        def _():
            load(i).wait()

        @pl.when(c > 0)
        def _():
            own_part(i).wait_recv()

        piece_ref = part(own_ref, i)
        forward(even & (c + 2 < columns), piece_ref, piece_ref, own_send.at[0, i], own_recv.at[i], (r, c + 2))
        forward(even, piece_ref, piece_ref, own_send.at[1, i], own_recv.at[i], (r, c + 1))
        forward((r == 0) & even & (rows > 2), piece_ref, part(diag_ref, i), diag_send.at[0, i], diag_recv.at[i], (r + 2, c))
        forward((r == 0) & even, piece_ref, part(diag_ref, i), diag_send.at[1, i], diag_recv.at[i], (r + 1, c))
        keep = pltpu.make_async_copy(piece_ref, part(diag_ref, i), keep_sem.at[0, i])
        keeps.append((r == 0, keep))

        @pl.when(r == 0)
        def _():
            keep.start()

    for i in range(CHUNKS):
        diag_piece = part(diag_ref, i)
        incoming = send(diag_piece, diag_piece, diag_send.at[0, i], diag_recv.at[i], (other, c))

        @pl.when(r > 0)
        def _():
            incoming.wait_recv()

        forward((r > 0) & even & (x == 0) & (r + 2 < rows), diag_piece, diag_piece, diag_send.at[0, i], diag_recv.at[i], (r + 2, c))
        forward((r > 0) & even & (x == 0), diag_piece, diag_piece, diag_send.at[1, i], diag_recv.at[i], (r + 1, c))
        forward((r > 0) & even, diag_piece, diag_piece, diag_send.at[2, i], diag_recv.at[i], (r, c + 1))

    for i in range(CHUNKS):
        target = part(cols_ref, i, base_x)

        def spread(condition, source):
            forward(condition & (q >= c) & (r + 2 < rows), source, target, cols_send.at[0, i], cols_recv.at[0, i], (r + 2, c))
            forward(condition & (q <= c) & (q > 0), source, target, cols_send.at[1, i], cols_recv.at[0, i], (r - 2, c))
            forward(condition, source, target, cols_send.at[2, i], cols_recv.at[1, i], (other, c))

        keep = pltpu.make_async_copy(part(own_ref, i), target, keep_sem.at[1, i])
        keeps.append((q == c, keep))

        @pl.when(q == c)
        def _():
            keep.start()

        spread(q == c, part(own_ref, i))
        incoming = send(target, target, cols_send.at[0, i], cols_recv.at[0, i], (other, c))

        @pl.when(q != c)
        def _():
            incoming.wait_recv()

        spread(q != c, target)

    for i in range(CHUNKS):
        target = part(cols_ref, i, base_o)
        send(target, target, cols_send.at[2, i], cols_recv.at[1, i], (other, c)).wait_recv()
    for condition, copy in sends:
        @pl.when(condition)
        def _():
            copy.wait_send()
    for condition, copy in keeps:
        @pl.when(condition)
        def _():
            copy.wait()


def gather(mine):
    width = mine.shape[0]
    square = jax.ShapeDtypeStruct((width, width), jnp.float32)
    dma = pltpu.SemaphoreType.DMA
    return pl.pallas_call(
        gather_kernel,
        out_shape=(square, square, jax.ShapeDtypeStruct((2 * width, width), jnp.float32)),
        in_specs=[pl.BlockSpec(memory_space=pl.ANY)],
        out_specs=(VMEM, VMEM, VMEM),
        scratch_shapes=[
            dma((CHUNKS,)), dma((2, CHUNKS)), dma((CHUNKS,)), dma((3, CHUNKS)), dma((CHUNKS,)),
            dma((3, CHUNKS)), dma((2, CHUNKS)), dma((2, CHUNKS)),
        ],
        compiler_params=pltpu.CompilerParams(collective_id=0, has_side_effects=True),
    )(mine)


def per_device(mine):
    own, diag, cols = gather(mine)
    l, w, logdet = cholesky(diag)
    block = pl.pallas_call(
        update_kernel,
        out_shape=jax.ShapeDtypeStruct(mine.shape, jnp.float32),
        in_specs=[VMEM] * 5,
        out_specs=VMEM,
    )(mine, own, cols, w, l)
    return block, logdet[0, 0]


def solution(mesh):
    return jax.shard_map(
        per_device, mesh=mesh, in_specs=(P("row", "col"),), out_specs=(P("row", "col"), P()), check_vma=False
    )
```

profile of v0, /device:TPU:7, one launch (start us, length us, event | category | flops | bytes accessed | tf_op | source)
XLA Modules:
  0.0 111.5 jit_solution(5752650292674734963)
XLA Ops:
  0.6 72.2 %shard_map.30 = (f32[512,512]{1,0:T(8,128)}, f32[512,512]{1,0:T(8,128)}, f32[1024,512]{1,0:T(8,128)}) custom-call(f32[512,1024]{1,0:T(8,128)} %mine_ref.3), custom_call_target="tpu_custom_call" | custom-call | tf_op jit(solution)/shard_map/pallas_call | solution.py:287
  72.8 25.3 %shard_map.31 = (f32[512,512]{1,0:T(8,128)}, f32[512,512]{1,0:T(8,128)}, f32[1,128]{1,0:T(1,128)}) custom-call(f32[512,512]{1,0:T(8,128)} %get-tuple-element.10.a_ref), custom_call_target="tpu_custom_call" | custom-call | tf_op jit(solution)/shard_map/pallas_call | solution.py:115
  98.1 13.3 %shard_map.32 = f32[512,1024]{1,0:T(8,128)} custom-call(f32[512,1024]{1,0:T(8,128)} %mine_ref.3, f32[512,512]{1,0:T(8,128)} %get-tuple-element.8.own_ref, f32[1024,512]{1,0:T(8,128)} %get-tuple-element.9.cols_ref, f32[512,512]{1,0:T(8,128)} %get-tuple-element.11.w_ref, f32[512,512]{1,0:T(8,128)} %get-tuple-element.12.l_ref), custom_call_target="tpu_custom_call" | custom-call | tf_op jit(solution)/shard_map/pallas_call | solution.py:303
where the time goes:
time: 112 us; the launch traced here: 111 us
  Pallas kernels  111 us (99%)
    pallas_call x1, Pallas kernels, gather(): pl.pallas_call(gather_kernel, out_shape=(square, square, jax.ShapeDtypeSt...  72.2 us
    pallas_call x1, Pallas kernels, cholesky(): pl.pallas_call(cholesky_kernel, out_shape=(square, square, jax.ShapeDtype...  25.3 us
    pallas_call x1, Pallas kernels, per_device(): pl.pallas_call(update_kernel, out_shape=jax.ShapeDtypeStruct(mine.shape,...  13.3 us

commit v1 on v0

--- a/solution.py
+++ b/solution.py
@@ -9,7 +9,7 @@
 
 MESH = pl.DeviceIdType.MESH
 NB = 128
-CHUNKS = 4
+CHUNKS = 8
 VMEM = pl.BlockSpec(memory_space=pltpu.VMEM)
 
 
@@ -27,7 +27,27 @@
     )
 
 
-def factor_block(a):
+def split(a):
+    high = a.astype(jnp.bfloat16)
+    return high, (a - high.astype(jnp.float32)).astype(jnp.bfloat16)
+
+
+def dot_nt_split(a, b):
+    def dot(u, v):
+        return lax.dot_general(u, v, (((1,), (1,)), ((), ())), preferred_element_type=jnp.float32)
+
+    return dot(a[0], b[0]) + (dot(a[0], b[1]) + dot(a[1], b[0]))
+
+
+def solve(rows, w_ref):
+    size = w_ref.shape[0]
+    half = size // 2
+    return jnp.concatenate(
+        [dot_nt(rows[:, : e], w_ref[e - half : e, :e]) for e in range(half, size + 1, half)], axis=1
+    )
+
+
+def factor_block(a, hook):
     groups = NB // 8
     lane = lax.broadcasted_iota(jnp.int32, (8, NB), 1)
     sub = lax.broadcasted_iota(jnp.int32, (8, NB), 0)
@@ -42,6 +62,8 @@
         return jnp.broadcast_to(x[:, t : t + 1], (8, NB))
 
     for p in range(groups):
+        if p == groups // 2:
+            hook()
         first = 8 * p
         v, i = left[p], right[p]
         cols = [column(v, first + t) for t in range(8)]
@@ -77,21 +99,23 @@
     return jnp.concatenate(upper, 0), jnp.concatenate(inverse, 0), jnp.concatenate(pivots, 0)
 
 
-def cholesky_kernel(a_ref, l_ref, w_ref, logdet_ref, work, upper, inverse, pivot):
+def factor_all(a_ref, l_ref, w_ref, logdet_ref, work, upper, inverse, pivot, relay):
     size = a_ref.shape[0]
-    work[...] = a_ref[...]
+    for end in range(NB, size + 1, NB):
+        work[end - NB : end, :end] = a_ref[end - NB : end, :end]
     l_ref[...] = jnp.zeros_like(l_ref)
     w_ref[...] = jnp.zeros_like(w_ref)
 
     @pl.loop(0, size // NB)
     def _(step):
         span = pl.ds(pl.multiple_of(step * NB, NB), NB)
-        r, w, d = factor_block(work[span, span])
+        r, w, d = factor_block(work[span, span], lambda: relay(2 * step))
         upper[...] = r
         inverse[...] = w
         pivot[span, :] = d
         w_ref[span, span] = inverse[...]
         l_ref[span, span] = upper[...].T
+        relay(2 * step + 1)
         for p in range(size // NB):
 
             @pl.when(step == p)
@@ -104,26 +128,11 @@
                 if end < size:
                     panel = dot_nt(work[end:, at], inverse[...])
                     l_ref[end:, at] = panel
-                    work[end:, end:] = work[end:, end:] - dot_nt(panel, panel)
+                    for col in range(end, size, NB):
+                        block = panel[col - end : col - end + NB, :]
+                        work[col:, col : col + NB] = work[col:, col : col + NB] - dot_nt(panel[col - end :, :], block)
 
     logdet_ref[...] = jnp.sum(jnp.log(pivot[...]), axis=0, keepdims=True)
-
-
-def cholesky(a):
-    size = a.shape[0]
-    square = jax.ShapeDtypeStruct((size, size), jnp.float32)
-    return pl.pallas_call(
-        cholesky_kernel,
-        out_shape=(square, square, jax.ShapeDtypeStruct((1, NB), jnp.float32)),
-        in_specs=[VMEM],
-        out_specs=(VMEM, VMEM, VMEM),
-        scratch_shapes=[
-            pltpu.VMEM((size, size), jnp.float32),
-            pltpu.VMEM((NB, NB), jnp.float32),
-            pltpu.VMEM((NB, NB), jnp.float32),
-            pltpu.VMEM((size, NB), jnp.float32),
-        ],
-    )(a)
 
 
 def update_kernel(mine_ref, own_ref, cols_ref, w_ref, l_ref, out_ref):
@@ -140,19 +149,20 @@
 
     @pl.when(r > 0)
     def _():
-        panel = dot_nt(own_ref[...], w_ref[...])
+        panel = solve(own_ref[...], w_ref)
+        panel_split = split(panel)
         for slot in range(2):
             at = slice(slot * width, (slot + 1) * width)
-            other = dot_nt(cols_ref[at, :], w_ref[...])
-            out_ref[:, at] = mine_ref[:, at] - dot_nt(panel, other)
+            other = solve(cols_ref[at, :], w_ref)
+            out_ref[:, at] = mine_ref[:, at] - dot_nt_split(panel_split, split(other))
 
         @pl.when(c == 0)
         def _():
             out_ref[:, :width] = panel
 
 
-def gather_kernel(mine_ref, own_ref, diag_ref, cols_ref, load_sem, own_send, own_recv,
-                  diag_send, diag_recv, cols_send, cols_recv, keep_sem):
+def panel_kernel(mine_ref, own_ref, cols_ref, l_ref, w_ref, logdet_ref, diag_ref, work, upper, inverse, pivot,
+                 load_sem, own_send, own_recv, diag_send, diag_recv, cols_send, cols_recv, keep_sem):
     rows, columns = lax.axis_size("row"), lax.axis_size("col")
     r, c = lax.axis_index("row"), lax.axis_index("col")
     q, x = r // 2, r % 2
@@ -176,7 +186,11 @@
     pl.semaphore_wait(barrier, peers)
 
     def part(ref, i, base=0):
-        return ref.at[pl.ds(base + i * piece, piece), :]
+        return ref.at[pl.ds(pl.multiple_of(base + i * piece, piece), piece), :]
+
+    def low(ref, i):
+        seen = -(-((i + 1) * piece) // NB) * NB
+        return ref.at[pl.ds(i * piece, piece), pl.ds(0, seen)]
 
     def send(source, target, send_sem, recv_sem, device):
         return pltpu.make_async_remote_copy(
@@ -201,6 +215,29 @@
         def _():
             copy.start()
 
+    def spread(i, source):
+        target = part(cols_ref, i, base_x)
+        return [
+            ((q >= c) & (r + 2 < rows), send(source, target, cols_send.at[0, i], cols_recv.at[0, i], (r + 2, c))),
+            ((q <= c) & (q > 0), send(source, target, cols_send.at[1, i], cols_recv.at[0, i], (r - 2, c))),
+            (q >= 0, send(source, target, cols_send.at[2, i], cols_recv.at[1, i], (other, c))),
+        ]
+
+    def start(condition, copies):
+        for exists, copy in copies:
+            @pl.when(condition & exists)
+            def _():
+                copy.start()
+
+    def relay(i):
+        target = part(cols_ref, i, base_x)
+
+        @pl.when(q != c)
+        def _():
+            send(target, target, cols_send.at[0, i], cols_recv.at[0, i], (other, c)).wait_recv()
+
+        start(q != c, spread(i, target))
+
     def own_part(i):
         return send(part(own_ref, i), part(own_ref, i), own_send.at[0, i], own_recv.at[i], (r, c + 1))
 
@@ -222,17 +259,25 @@
         piece_ref = part(own_ref, i)
         forward(even & (c + 2 < columns), piece_ref, piece_ref, own_send.at[0, i], own_recv.at[i], (r, c + 2))
         forward(even, piece_ref, piece_ref, own_send.at[1, i], own_recv.at[i], (r, c + 1))
-        forward((r == 0) & even & (rows > 2), piece_ref, part(diag_ref, i), diag_send.at[0, i], diag_recv.at[i], (r + 2, c))
-        forward((r == 0) & even, piece_ref, part(diag_ref, i), diag_send.at[1, i], diag_recv.at[i], (r + 1, c))
-        keep = pltpu.make_async_copy(piece_ref, part(diag_ref, i), keep_sem.at[0, i])
-        keeps.append((r == 0, keep))
+        low_ref = low(own_ref, i)
+        forward((r == 0) & even & (rows > 2), low_ref, low(diag_ref, i), diag_send.at[0, i], diag_recv.at[i], (r + 2, c))
+        forward((r == 0) & even, low_ref, low(diag_ref, i), diag_send.at[1, i], diag_recv.at[i], (r + 1, c))
+        keep = pltpu.make_async_copy(low_ref, low(diag_ref, i), keep_sem.at[0, i])
 
         @pl.when(r == 0)
         def _():
             keep.start()
 
-    for i in range(CHUNKS):
-        diag_piece = part(diag_ref, i)
+        start(q == c, spread(i, piece_ref))
+        keep_cols = pltpu.make_async_copy(piece_ref, part(cols_ref, i, base_x), keep_sem.at[1, i])
+        keeps.append((q == c, keep_cols))
+
+        @pl.when(q == c)
+        def _():
+            keep_cols.start()
+
+    for i in range(CHUNKS):
+        diag_piece = low(diag_ref, i)
         incoming = send(diag_piece, diag_piece, diag_send.at[0, i], diag_recv.at[i], (other, c))
 
         @pl.when(r > 0)
@@ -244,32 +289,17 @@
         forward((r > 0) & even, diag_piece, diag_piece, diag_send.at[2, i], diag_recv.at[i], (r, c + 1))
 
     for i in range(CHUNKS):
-        target = part(cols_ref, i, base_x)
-
-        def spread(condition, source):
-            forward(condition & (q >= c) & (r + 2 < rows), source, target, cols_send.at[0, i], cols_recv.at[0, i], (r + 2, c))
-            forward(condition & (q <= c) & (q > 0), source, target, cols_send.at[1, i], cols_recv.at[0, i], (r - 2, c))
-            forward(condition, source, target, cols_send.at[2, i], cols_recv.at[1, i], (other, c))
-
-        keep = pltpu.make_async_copy(part(own_ref, i), target, keep_sem.at[1, i])
-        keeps.append((q == c, keep))
-
-        @pl.when(q == c)
-        def _():
-            keep.start()
-
-        spread(q == c, part(own_ref, i))
-        incoming = send(target, target, cols_send.at[0, i], cols_recv.at[0, i], (other, c))
-
-        @pl.when(q != c)
-        def _():
-            incoming.wait_recv()
-
-        spread(q != c, target)
+        @pl.when(r == 0)
+        def _():
+            pltpu.make_async_copy(low(own_ref, i), low(diag_ref, i), keep_sem.at[0, i]).wait()
+
+    factor_all(diag_ref, l_ref, w_ref, logdet_ref, work, upper, inverse, pivot, relay)
 
     for i in range(CHUNKS):
         target = part(cols_ref, i, base_o)
         send(target, target, cols_send.at[2, i], cols_recv.at[1, i], (other, c)).wait_recv()
+    for i in range(CHUNKS):
+        sends += spread(i, part(cols_ref, i, base_x))
     for condition, copy in sends:
         @pl.when(condition)
         def _():
@@ -280,16 +310,22 @@
             copy.wait()
 
 
-def gather(mine):
+def panel_step(mine):
     width = mine.shape[0]
     square = jax.ShapeDtypeStruct((width, width), jnp.float32)
     dma = pltpu.SemaphoreType.DMA
     return pl.pallas_call(
-        gather_kernel,
-        out_shape=(square, square, jax.ShapeDtypeStruct((2 * width, width), jnp.float32)),
+        panel_kernel,
+        out_shape=(
+            square, jax.ShapeDtypeStruct((2 * width, width), jnp.float32), square, square,
+            jax.ShapeDtypeStruct((1, NB), jnp.float32),
+        ),
         in_specs=[pl.BlockSpec(memory_space=pl.ANY)],
-        out_specs=(VMEM, VMEM, VMEM),
+        out_specs=(VMEM,) * 5,
         scratch_shapes=[
+            pltpu.VMEM((width, width), jnp.float32), pltpu.VMEM((width, width), jnp.float32),
+            pltpu.VMEM((NB, NB), jnp.float32), pltpu.VMEM((NB, NB), jnp.float32),
+            pltpu.VMEM((width, NB), jnp.float32),
             dma((CHUNKS,)), dma((2, CHUNKS)), dma((CHUNKS,)), dma((3, CHUNKS)), dma((CHUNKS,)),
             dma((3, CHUNKS)), dma((2, CHUNKS)), dma((2, CHUNKS)),
         ],
@@ -298,8 +334,7 @@
 
 
 def per_device(mine):
-    own, diag, cols = gather(mine)
-    l, w, logdet = cholesky(diag)
+    own, cols, l, w, logdet = panel_step(mine)
     block = pl.pallas_call(
         update_kernel,
         out_shape=jax.ShapeDtypeStruct(mine.shape, jnp.float32),

time: 112 us -> 81.2 us (0.72)
  Pallas kernels: 111 us -> 79.3 us
  between operations: 0.64 us -> 1.81 us
    pallas_call x2 -> x1, Pallas kernels: 97.5 us -> 66.7 us  [panel_step(): pl.pallas_call(panel_kernel, out_shape=(square, jax.ShapeDtypeStruct((2 *...]
where the time goes in v1:
time: 81.2 us; the launch traced here: 81.1 us
  Pallas kernels  79.3 us (98%)
  between operations  1.81 us (2%)
    pallas_call x1, Pallas kernels, panel_step(): pl.pallas_call(panel_kernel, out_shape=(square, jax.ShapeDtypeStruct((2 *...  66.7 us
    pallas_call x1, Pallas kernels, per_device(): pl.pallas_call(update_kernel, out_shape=jax.ShapeDtypeStruct(mine.shape,...  12.6 us

profile of v1, /device:TPU:7, one launch (start us, length us, event | category | flops | bytes accessed | tf_op | source)
XLA Modules:
  0.0 81.1 jit_solution(6522351370606335918)
XLA Ops:
  0.6 66.7 %shard_map.30 = (f32[512,512]{1,0:T(8,128)}, f32[1024,512]{1,0:T(8,128)}, f32[512,512]{1,0:T(8,128)}, f32[512,512]{1,0:T(8,128)}, f32[1,128]{1,0:T(1,128)}) custom-call(f32[512,1024]{1,0:T(8,128)} %mine_ref.3), custom_call_target="tpu_custom_call" | custom-call | tf_op jit(solution)/shard_map/pallas_call | solution.py:317
  67.3 0.0 copy-start
  67.3 12.6 %shard_map.31 = f32[512,1024]{1,0:T(8,128)} custom-call(f32[512,1024]{1,0:T(8,128)} %mine_ref.3, f32[512,512]{1,0:T(8,128)} %get-tuple-element.7.own_ref, f32[1024,512]{1,0:T(8,128)} %get-tuple-element.8.cols_ref, f32[512,512]{1,0:T(8,128)} %get-tuple-element.9.w_ref, f32[512,512]{1,0:T(8,128)} %get-tuple-element.10.l_ref), custom_call_target="tpu_custom_call" | custom-call | tf_op jit(solution)/shard_map/pallas_call | solution.py:338
  79.9 0.0 copy-done
Async XLA Ops:
  67.3 12.6 %copy-start = (f32[1,128]{1,0:T(1,128)S(1)}, f32[1,128]{1,0:T(1,128)}, u32[]{:S(2)}) copy-start(f32[1,128]{1,0:T(1,128)} %get-tuple-element.11) | copy-start | bytes 1540
